TPU v7x, 32 devices: a whole 2x2x4 slice. The times are simulated.
32 devices in a mesh: wav: 8 (over y, x, core), lev: 4 (over z).
Axes of the slice: x: 2, y: 2, z: 4, core: 2. Of those that a mesh axis runs over, the one named last changes fastest.
Arguments:
- spectral: bfloat16 [200, 401, 512], P('wav', None, 'lev'), may hold values from -0.1796875 to 0.1796875
- legendre: bfloat16 [200, 401, 64], P('wav', None, 'lev'), may hold values from -0.4375 to 0.4375
- wave_pair: int32 [200], replicated, may hold values from -1 to 199, as said below
- lat_slot: int32 [64], replicated, may hold values from 0 to 799, as said below
Outputs:
- gridded: bfloat16 [64, 256, 1616], P('wav', 'lev')
Inputs may be any that keep to these rules, and one draw needn't show every extreme that they name: `wave_pair`: each pair number 0 to 199 appears exactly once; all other entries are -1. `lat_slot`: the entries are distinct latitudes.
All inputs are finite; a program needn't handle non-finite values.
Results may differ from a plain program's by a relative error of at most 0.0055.
Values may be sent and summed in bfloat16 or wider, within the bound.
A program may use at most 64 MiB of HBM per device.

v0:
```python
import math

import jax
import jax.numpy as jnp
from jax import lax
from jax.sharding import PartitionSpec as P

NLAT = 800


def fold_masks(pair_ids, fold_count, wave_count):
    fold_rows = jnp.arange(fold_count, dtype=jnp.int32)
    filled = pair_ids >= 0
    border = wave_count - pair_ids
    lower = filled[:, None] & (fold_rows[None, :] < border[:, None])
    upper = filled[:, None] & (fold_rows[None, :] >= border[:, None])
    return jnp.stack([lower, upper], axis=1)


def trig_parts(wave_numbers, steps, counts_b):
    residue = wave_numbers[None, None] * steps[None, :, None, None] % counts_b
    angles = residue.astype(jnp.float32) * (2.0 * math.pi) / counts_b.astype(jnp.float32)
    return (jnp.cos(angles), jnp.sin(angles))


def synthesis_table(pair_ids, row_lats, lat_count, lon_width, wave_count):
    filled = pair_ids >= 0
    wave_numbers = jnp.stack([pair_ids, wave_count - 1 - pair_ids], axis=1)
    lon_count = 20 + 4 * jnp.minimum(row_lats, lat_count - 1 - row_lats)
    highest = jnp.minimum(wave_count - 1, (lon_count - 1) // 2)
    counts_b = lon_count[:, None, None, None]
    coarse_count = (lon_width + 63) // 64
    coarse_steps = jnp.arange(coarse_count, dtype=jnp.int32) * 64
    fine_steps = jnp.arange(64, dtype=jnp.int32)
    cos_coarse, sin_coarse = trig_parts(wave_numbers, coarse_steps, counts_b)
    cos_fine, sin_fine = trig_parts(wave_numbers, fine_steps, counts_b)
    cos_all = (
        cos_coarse[:, :, None] * cos_fine[:, None] - sin_coarse[:, :, None] * sin_fine[:, None]
    )
    sin_all = (
        sin_coarse[:, :, None] * cos_fine[:, None] + cos_coarse[:, :, None] * sin_fine[:, None]
    )
    row_total = row_lats.shape[0]
    cos_all = cos_all.reshape(row_total, coarse_count * 64, wave_numbers.shape[0], 2)[:, :lon_width]
    sin_all = sin_all.reshape(row_total, coarse_count * 64, wave_numbers.shape[0], 2)[:, :lon_width]
    columns = jnp.arange(lon_width, dtype=jnp.int32)
    valid = (
        filled[None, None, :, None]
        & (wave_numbers[None, None] <= highest[:, None, None, None])
        & (columns[None, :, None, None] < counts_b)
    )
    factor = jnp.where(wave_numbers == 0, 1.0, 2.0).astype(jnp.float32)[None, None]
    real_part = jnp.where(valid, factor * cos_all, 0.0)
    imag_part = jnp.where(valid, -factor * sin_all, 0.0)
    return jnp.stack([real_part, imag_part], axis=-1).astype(jnp.bfloat16)


def legendre_sum(coefficients, weights, half_masks):
    paired = coefficients.reshape(
        coefficients.shape[0], coefficients.shape[1], coefficients.shape[2] // 2, 2
    )
    masked = jnp.where(
        half_masks[:, :, :, None, None], paired[:, None], jnp.zeros((), paired.dtype)
    )
    summed = jnp.einsum("shtlc,sta->ashcl", masked, weights, preferred_element_type=jnp.float32)
    return summed.astype(jnp.bfloat16)


def on_device(spectral, legendre, wave_pair, lat_slot):
    slot_count = spectral.shape[0]
    fold_count = spectral.shape[1]
    wave_count = fold_count - 1
    lat_count = NLAT
    lon_width = 2 * lat_count + 16
    wav_devices = lax.axis_size("wav")
    wav_index = lax.axis_index("wav")
    own_pairs = lax.dynamic_slice_in_dim(wave_pair, wav_index * slot_count, slot_count)
    half_masks = fold_masks(own_pairs, fold_count, wave_count)
    fourier = legendre_sum(
        spectral, lax.all_gather(legendre, "lev", axis=2, tiled=True), half_masks
    )
    row_count = lat_slot.shape[0] // wav_devices
    row_lats = lax.dynamic_slice_in_dim(lat_slot, wav_index * row_count, row_count)
    group_rows = max(1, row_count // 25)
    while row_count % group_rows:
        group_rows -= 1
    group_count = row_count // group_rows
    received = lax.all_to_all(fourier, "wav", split_axis=0, concat_axis=1, tiled=True)
    layer_items = received.shape[4]
    grouped = received.reshape((group_count, group_rows) + received.shape[1:])
    lat_groups = row_lats.reshape(group_count, group_rows)

    def one_group(args):
        values, group_lats = args
        basis = synthesis_table(wave_pair, group_lats, lat_count, lon_width, wave_count)
        result = jnp.einsum("rjghc,rghcl->rlj", basis, values, preferred_element_type=jnp.float32)
        return result.astype(jnp.bfloat16)

    gridded_groups = lax.map(one_group, (grouped, lat_groups))
    return gridded_groups.reshape(row_count, layer_items, lon_width)


def solution(mesh):
    return jax.shard_map(
        on_device,
        mesh=mesh,
        in_specs=(P("wav", None, "lev"), P("wav", None, "lev"), P(), P()),
        out_specs=P("wav", "lev", None),
        check_vma=False,
    )
```

profile of v0, /device:TPU:1, one launch (start us, length us, event | category | flops | bytes accessed | tf_op | source)
XLA Modules:
  0.0 254.4 jit_solution(4773059625746741273)
XLA Ops:
  7.3 5.4 %copy.16 = bf16[25,401,128]{1,2,0:T(8,128)(2,1)} copy(bf16[25,401,128]{2,1,0:T(8,128)(2,1)} %param.6) | data formatting | bytes 5132800 | tf_op args[0]
  12.7 6.7 %broadcast_in_dim.92 = bf16[25,401,64,2]{1,3,2,0:T(2,128)(2,1)S(1)} reshape(bf16[25,401,128]{1,2,0:T(8,128)(2,1)} %copy.16) | data formatting | bytes 5132800 | tf_op jit(solution)/shard_map/jit(_where)/broadcast_in_dim | solution.py:62
  19.4 2.4 copy.17
  22.3 26.3 %all-gather.2.cloned.1.call-done = bf16[25,401,64]{1,2,0:T(8,128)(2,1)} async-done(((bf16[25,401,16]{1,2,0:T(8,128)(2,1)}), bf16[25,401,64]{1,2,0:T(8,128)(2,1)}) %all-gather.2.cloned.1.call-update) | async-done | bytes 1283216 | tf_op jit(solution)/shard_map/all_gather | solution.py:80
  48.7 4.3 %fusion.52 = bf16[64,25,2,2,64]{0,4,3,2,1:T(8,128)(2,1)S(1)} fusion(bf16[25,401,64]{1,2,0:T(8,128)(2,1)} %all-gather.2.cloned.1.call-done, pred[25,2,401]{2,1,0:T(4,128)(4,1)S(1)} %pad_add_fusion.1, bf16[25,401,64,2]{1,2,3,0:T(8,128)(2,1)} %copy.17), kind=kOutput, calls=%fused_computation.59 | convolution fusion | flops 331475200 | bytes 4688850 | tf_op jit(solution)/shard_map/shtlc,sta->ashcl/dot_general | solution.py:65
  52.9 3.0 %copy.18 = bf16[64,25,2,2,64]{4,3,2,1,0:T(2,128)(2,1)S(1)} copy(bf16[64,25,2,2,64]{0,4,3,2,1:T(8,128)(2,1)S(1)} %fusion.52) | data formatting | bytes 1638400 | tf_op jit(solution)/shard_map/convert_element_type | solution.py:66
  55.9 1.8 reshape.584
  57.7 4.8 %all-to-all-start = ((bf16[8,2,25600]{2,1,0:T(2,128)(2,1)}), bf16[8,2,25600]{2,1,0:T(2,128)(2,1)S(1)}, u32[]{:S(2)}, u32[]{:S(2)}) async-start(bf16[8,2,25600]{2,1,0:T(2,128)(2,1)} %reshape.584), calls=%async_computation | async-start | bytes 1638400 | tf_op jit(solution)/shard_map/all_to_all | solution.py:88
  62.6 9.4 %all-to-all-done = bf16[8,2,25600]{2,1,0:T(2,128)(2,1)S(1)} async-done(((bf16[8,2,25600]{2,1,0:T(2,128)(2,1)}), bf16[8,2,25600]{2,1,0:T(2,128)(2,1)S(1)}, u32[]{:S(2)}, u32[]{:S(2)}) %all-to-all-start) | async-done | bytes 819232 | tf_op jit(solution)/shard_map/all_to_all | solution.py:88
  73.7 2.4 copy.21
  76.1 171.5 %while.15 = (s32[]{:T(128)}, bf16[8,1,64,1616]{3,2,1,0:T(8,128)(2,1)}, bf16[8,1,200,2,2,64]{2,5,3,4,1,0:T(8,128)(2,1)}, s32[200]{0:T(256)S(1)}, s32[8,1]{0,1:T(1...) while((s32[]{:T(128)}, ...), condition=%wide.region_1.2_spmd, body=%wide.region_0.1_spmd.sunk | while | flops 175794288 | bytes 47638996 | solution.py:99
  78.0 1.8 fusion.66
  81.6 1.9 slice.24
  83.5 3.5 %copy.30 = f32[1,1616,200,2]{1,2,3,0:T(8,128)} copy(f32[1,1616,200,2]{2,1,3,0:T(8,128)} %slice.24) | data formatting | bytes 5171200 | tf_op jit(solution)/shard_map/while
  87.1 1.9 slice.25
  89.0 3.7 %copy.31 = f32[1,1616,200,2]{1,2,3,0:T(8,128)} copy(f32[1,1616,200,2]{2,1,3,0:T(8,128)} %slice.25) | data formatting | bytes 5171200 | tf_op jit(solution)/shard_map/while
  92.8 2.5 fusion.68
  95.3 2.3 fusion.69
  99.5 1.8 fusion.66
  103.0 1.9 slice.24
  104.9 3.5 %copy.30 = f32[1,1616,200,2]{1,2,3,0:T(8,128)} copy(f32[1,1616,200,2]{2,1,3,0:T(8,128)} %slice.24) | data formatting | bytes 5171200 | tf_op jit(solution)/shard_map/while
  108.5 1.9 slice.25
  110.4 3.7 %copy.31 = f32[1,1616,200,2]{1,2,3,0:T(8,128)} copy(f32[1,1616,200,2]{2,1,3,0:T(8,128)} %slice.25) | data formatting | bytes 5171200 | tf_op jit(solution)/shard_map/while
  114.2 2.5 fusion.68
  116.7 2.3 fusion.69
  120.9 1.8 fusion.66
  124.5 1.9 slice.24
  126.4 3.5 %copy.30 = f32[1,1616,200,2]{1,2,3,0:T(8,128)} copy(f32[1,1616,200,2]{2,1,3,0:T(8,128)} %slice.24) | data formatting | bytes 5171200 | tf_op jit(solution)/shard_map/while
  129.9 1.9 slice.25
  131.8 3.7 %copy.31 = f32[1,1616,200,2]{1,2,3,0:T(8,128)} copy(f32[1,1616,200,2]{2,1,3,0:T(8,128)} %slice.25) | data formatting | bytes 5171200 | tf_op jit(solution)/shard_map/while
  135.6 2.5 fusion.68
  138.1 2.3 fusion.69
  142.3 1.8 fusion.66
  145.9 1.9 slice.24
  147.8 3.5 %copy.30 = f32[1,1616,200,2]{1,2,3,0:T(8,128)} copy(f32[1,1616,200,2]{2,1,3,0:T(8,128)} %slice.24) | data formatting | bytes 5171200 | tf_op jit(solution)/shard_map/while
  151.4 1.9 slice.25
  153.3 3.7 %copy.31 = f32[1,1616,200,2]{1,2,3,0:T(8,128)} copy(f32[1,1616,200,2]{2,1,3,0:T(8,128)} %slice.25) | data formatting | bytes 5171200 | tf_op jit(solution)/shard_map/while
  157.1 2.5 fusion.68
  159.6 2.3 fusion.69
  163.8 1.8 fusion.66
  167.3 1.9 slice.24
  169.2 3.5 %copy.30 = f32[1,1616,200,2]{1,2,3,0:T(8,128)} copy(f32[1,1616,200,2]{2,1,3,0:T(8,128)} %slice.24) | data formatting | bytes 5171200 | tf_op jit(solution)/shard_map/while
  172.8 1.9 slice.25
  174.7 3.7 %copy.31 = f32[1,1616,200,2]{1,2,3,0:T(8,128)} copy(f32[1,1616,200,2]{2,1,3,0:T(8,128)} %slice.25) | data formatting | bytes 5171200 | tf_op jit(solution)/shard_map/while
  178.5 2.5 fusion.68
  181.0 2.3 fusion.69
  188.8 1.9 slice.24
  190.7 3.5 %copy.30 = f32[1,1616,200,2]{1,2,3,0:T(8,128)} copy(f32[1,1616,200,2]{2,1,3,0:T(8,128)} %slice.24) | data formatting | bytes 5171200 | tf_op jit(solution)/shard_map/while
  194.2 1.9 slice.25
  196.1 3.7 %copy.31 = f32[1,1616,200,2]{1,2,3,0:T(8,128)} copy(f32[1,1616,200,2]{2,1,3,0:T(8,128)} %slice.25) | data formatting | bytes 5171200 | tf_op jit(solution)/shard_map/while
  199.9 2.5 fusion.68
  202.4 2.3 fusion.69
  210.2 1.9 slice.24
  212.1 3.5 %copy.30 = f32[1,1616,200,2]{1,2,3,0:T(8,128)} copy(f32[1,1616,200,2]{2,1,3,0:T(8,128)} %slice.24) | data formatting | bytes 5171200 | tf_op jit(solution)/shard_map/while
  215.7 1.9 slice.25
  217.6 3.7 %copy.31 = f32[1,1616,200,2]{1,2,3,0:T(8,128)} copy(f32[1,1616,200,2]{2,1,3,0:T(8,128)} %slice.25) | data formatting | bytes 5171200 | tf_op jit(solution)/shard_map/while
  221.4 2.5 fusion.68
  223.9 2.3 fusion.69
  231.6 1.9 slice.24
  233.5 3.5 %copy.30 = f32[1,1616,200,2]{1,2,3,0:T(8,128)} copy(f32[1,1616,200,2]{2,1,3,0:T(8,128)} %slice.24) | data formatting | bytes 5171200 | tf_op jit(solution)/shard_map/while
  237.1 1.9 slice.25
  239.0 3.7 %copy.31 = f32[1,1616,200,2]{1,2,3,0:T(8,128)} copy(f32[1,1616,200,2]{2,1,3,0:T(8,128)} %slice.25) | data formatting | bytes 5171200 | tf_op jit(solution)/shard_map/while
  242.8 2.5 fusion.68
  245.3 2.3 fusion.69
  (114 shorter events, 27.9 us)
Async XLA Ops:
  6.5 56.0 %copy-start = (s32[64]{0:T(128)S(1)}, s32[64]{0:T(128)}, u32[]{:S(2)}) copy-start(s32[64]{0:T(128)} %param.9) | copy-start | bytes 772
  6.5 42.1 %all-gather.2.cloned.1.call-start = ((), (), s32[]{:S(2)}) async-start(), calls=%async_computation.1 | async-start | bytes 2048000 | tf_op jit(solution)/shard_map/all_gather | solution.py:80
  19.4 2.4 copy-start.2
  57.7 14.3 %all-to-all-start = ((bf16[8,2,25600]{2,1,0:T(2,128)(2,1)}), bf16[8,2,25600]{2,1,0:T(2,128)(2,1)S(1)}, u32[]{:S(2)}, u32[]{:S(2)}) async-start(bf16[8,2,25600]{2,1,0:T(2,128)(2,1)} %reshape.584), calls=%async_computation | async-start | bytes 1638400 | tf_op jit(solution)/shard_map/all_to_all | solution.py:88
  89.0 3.8 %copy-start.1 = (f32[1,1616,200,2]{1,2,3,0:T(8,128)S(1)}, f32[1,1616,200,2]{1,2,3,0:T(8,128)}, u32[]{:S(2)}) copy-start(f32[1,1616,200,2]{1,2,3,0:T(8,128)} %copy.30) | copy-start | bytes 7756804 | tf_op jit(solution)/shard_map/while
  110.4 3.8 %copy-start.1 = (f32[1,1616,200,2]{1,2,3,0:T(8,128)S(1)}, f32[1,1616,200,2]{1,2,3,0:T(8,128)}, u32[]{:S(2)}) copy-start(f32[1,1616,200,2]{1,2,3,0:T(8,128)} %copy.30) | copy-start | bytes 7756804 | tf_op jit(solution)/shard_map/while
  131.8 3.8 %copy-start.1 = (f32[1,1616,200,2]{1,2,3,0:T(8,128)S(1)}, f32[1,1616,200,2]{1,2,3,0:T(8,128)}, u32[]{:S(2)}) copy-start(f32[1,1616,200,2]{1,2,3,0:T(8,128)} %copy.30) | copy-start | bytes 7756804 | tf_op jit(solution)/shard_map/while
  153.3 3.8 %copy-start.1 = (f32[1,1616,200,2]{1,2,3,0:T(8,128)S(1)}, f32[1,1616,200,2]{1,2,3,0:T(8,128)}, u32[]{:S(2)}) copy-start(f32[1,1616,200,2]{1,2,3,0:T(8,128)} %copy.30) | copy-start | bytes 7756804 | tf_op jit(solution)/shard_map/while
  174.7 3.8 %copy-start.1 = (f32[1,1616,200,2]{1,2,3,0:T(8,128)S(1)}, f32[1,1616,200,2]{1,2,3,0:T(8,128)}, u32[]{:S(2)}) copy-start(f32[1,1616,200,2]{1,2,3,0:T(8,128)} %copy.30) | copy-start | bytes 7756804 | tf_op jit(solution)/shard_map/while
  196.1 3.8 %copy-start.1 = (f32[1,1616,200,2]{1,2,3,0:T(8,128)S(1)}, f32[1,1616,200,2]{1,2,3,0:T(8,128)}, u32[]{:S(2)}) copy-start(f32[1,1616,200,2]{1,2,3,0:T(8,128)} %copy.30) | copy-start | bytes 7756804 | tf_op jit(solution)/shard_map/while
  217.6 3.8 %copy-start.1 = (f32[1,1616,200,2]{1,2,3,0:T(8,128)S(1)}, f32[1,1616,200,2]{1,2,3,0:T(8,128)}, u32[]{:S(2)}) copy-start(f32[1,1616,200,2]{1,2,3,0:T(8,128)} %copy.30) | copy-start | bytes 7756804 | tf_op jit(solution)/shard_map/while
  239.0 3.8 %copy-start.1 = (f32[1,1616,200,2]{1,2,3,0:T(8,128)S(1)}, f32[1,1616,200,2]{1,2,3,0:T(8,128)}, u32[]{:S(2)}) copy-start(f32[1,1616,200,2]{1,2,3,0:T(8,128)} %copy.30) | copy-start | bytes 7756804 | tf_op jit(solution)/shard_map/while
Sparse Core Ops, SparseCore 0:
  8.9 39.7 all-gather.1
where the time goes:
time: 259 us; the launch traced here: 254 us
  local copies, waits for them, and re-layouts  117 us (45%)
  other arithmetic  49.3 us (19%)
  waiting for transfers between devices  36.4 us (14%)
  matrix products  22.6 us (9%)
  between operations  13.5 us (5%)
  loops' own time  10.7 us (4%)
  starting transfers between devices  4.79 us (2%)
    while x32, local copies, waits for them, and re-layouts  58.4 us
    all_gather x1, waiting for transfers between devices, on_device(): lax.all_gather(legendre, 'lev', axis=2, tiled=True)  26.3 us
    cos x16, other arithmetic, trig_parts(): return (jnp.cos(angles), jnp.sin(angles))  22.2 us
    another operation x8, other arithmetic, synthesis_table(): return jnp.stack([real_part, imag_part], axis=-1).astype(jnp.bfloat16)  19.9 us
    dot_general x8, matrix products, one_group(): jnp.einsum('rjghc,rghcl->rlj', basis, values, preferred_element_type=jnp....  18.3 us
    slice x8, local copies, waits for them, and re-layouts, synthesis_table(): cos_all.reshape(row_total, coarse_count * 64, wave_numbers.shape[0], 2)  15.2 us
    slice x8, local copies, waits for them, and re-layouts, synthesis_table(): sin_all.reshape(row_total, coarse_count * 64, wave_numbers.shape[0], 2)  15.2 us
    another operation x1, loops' own time, on_device(): gridded_groups = lax.map(one_group, (grouped, lat_groups))  10.7 us
  transfers between devices with their start and end apart: 2, of which 2 were waited for; matrix products, arithmetic and copies ran while one was open for 6% of the time, Pallas kernels for 0%

commit v1 on v0

v1 whole, which is shorter than its diff:
```python
import functools
import math

import jax
import jax.numpy as jnp
from jax import lax
from jax.experimental import pallas as pl
from jax.experimental.pallas import tpu as pltpu
from jax.sharding import PartitionSpec as P

NLAT = 800
CH = 16
LANE = 128
KB = 64


def half_turn(x):
    u = x * math.pi
    v = u * u
    s = -2.5052108385441720e-08
    for coef in (2.7557319223985893e-06, -1.9841269841269841e-04, 8.3333333333333333e-03, -1.6666666666666667e-01, 1.0):
        s = s * v + coef
    s = s * u
    c = -2.7557319223985888e-07
    for coef in (2.4801587301587302e-05, -1.3888888888888889e-03, 4.1666666666666667e-02, -0.5, 1.0):
        c = c * v + coef
    return 1.0 - 2.0 * s * s, 2.0 * s * c


def trig(prod, count, inv):
    r = prod - jnp.floor(prod * inv + 0.5) * count
    return half_turn(r * inv)


def kernel(
    nw, nl, slots, wave_count, half_width,
    wp_ref, lat_ref, meven_ref, perm_ref, spec_ref, leg_ref, out_ref,
    spec, leg, stage, snd, rcv, basis, obuf,
    loc_sem, ag_send, ag_recv, aa_send, aa_recv, own_sem, out_sem,
):
    wi = lax.axis_index("wav")
    li = lax.axis_index("lev")
    chunks = snd.shape[0]
    rows = obuf.shape[0]
    fold = spec.shape[1]
    layers = obuf.shape[1]
    width = out_ref.shape[2]
    kdim = chunks * nw * CH
    blocks = half_width // LANE
    qtot = nw * rows
    fmt = pl.DeviceIdType.MESH

    spec_copy = pltpu.make_async_copy(spec_ref, spec, loc_sem.at[0])
    spec_copy.start()
    leg_copy = pltpu.make_async_copy(leg_ref, leg.at[li], loc_sem.at[1])
    leg_copy.start()

    barrier = pltpu.get_barrier_semaphore()
    for d in range(1, nl):
        pl.semaphore_signal(barrier, inc=1, device_id=(wi, lax.rem(li + d, nl)), device_id_type=fmt)
    for d in range(1, nw):
        pl.semaphore_signal(barrier, inc=1, device_id=(lax.rem(wi + d, nw), li), device_id_type=fmt)
    pl.semaphore_wait(barrier, nl - 1 + nw - 1)

    def ag(c, d):
        lo, hi = c * CH, min(slots, (c + 1) * CH)
        return pltpu.make_async_remote_copy(
            src_ref=leg_ref.at[pl.ds(lo, hi - lo)],
            dst_ref=leg.at[li, pl.ds(lo, hi - lo)],
            send_sem=ag_send.at[c, d],
            recv_sem=ag_recv.at[c, d],
            device_id=(wi, lax.rem(li + d, nl)),
            device_id_type=fmt,
        )

    def aa(c, d):
        dest = lax.rem(wi + d, nw)
        return pltpu.make_async_remote_copy(
            src_ref=snd.at[c, dest],
            dst_ref=rcv.at[c, wi],
            send_sem=aa_send.at[c, d],
            recv_sem=aa_recv.at[c, d],
            device_id=(dest, li),
            device_id_type=fmt,
        )

    for c in range(chunks):
        for d in range(1, nl):
            ag(c, d).start()

    fine = lax.broadcasted_iota(jnp.int32, (KB, LANE), 1).astype(jnp.float32)

    def make_basis(step, carry):
        r = lax.div(step, kdim // KB)
        k0 = pl.multiple_of(lax.rem(step, kdim // KB) * KB, KB)
        lat = lat_ref[wi * rows + r]
        count_i = 20 + 4 * jnp.minimum(lat, NLAT - 1 - lat)
        highest = jnp.minimum(wave_count - 1, lax.shift_right_logical(count_i - 1, 1)).astype(jnp.float32)
        count = jnp.full((KB, LANE), count_i.astype(jnp.float32), jnp.float32)
        inv = 1.0 / count
        m_even = meven_ref[pl.ds(k0, KB), :]
        for par in range(2):
            m = m_even if par == 0 else (wave_count - 1.0) - m_even
            amp = jnp.where((m >= 0.0) & (m <= highest), jnp.where(m == 0.0, 1.0, 2.0), 0.0)
            cf, sf = trig(m * fine, count, inv)
            cc, sc = trig(m * (fine * LANE), count, inv)
            cc = cc * amp
            sc = sc * amp
            for b in range(blocks):
                cb = cc[:, b : b + 1]
                sb = sc[:, b : b + 1]
                cols = slice(b * LANE, (b + 1) * LANE)
                basis[r, par, pl.ds(k0, KB), cols] = (cb * cf - sb * sf).astype(jnp.bfloat16)
                basis[r, par, pl.ds(kdim + k0, KB), cols] = (-(sb * cf + cb * sf)).astype(jnp.bfloat16)
        return carry

    def basis_rows(lo, hi):
        lax.fori_loop(lo * (kdim // KB), hi * (kdim // KB), make_basis, 0)

    stage[...] = jnp.zeros_like(stage)
    cols = lax.broadcasted_iota(jnp.int32, (1, fold), 1)

    def fourier(c):
        lo, hi = c * CH, min(slots, (c + 1) * CH)

        def one(i, carry):
            s = lo + i
            p = wp_ref[wi * slots + s]
            low = jnp.where(cols < wave_count - p, 1, 0)
            par = jnp.bitwise_and(p, 1)
            even = jnp.where(low != par, 1.0, 0.0).astype(jnp.bfloat16)
            lg = leg[:, pl.ds(s, 1)].reshape(qtot, fold)
            lg_even = lg * even
            both = jnp.concatenate([lg_even, lg - lg_even], axis=0)
            f = jnp.dot(both, spec[s], preferred_element_type=jnp.float32).astype(jnp.bfloat16)
            g = jnp.dot(f, perm_ref[...], preferred_element_type=jnp.float32)
            for h in range(2):
                stage[pl.ds(h * CH + i, qtot, stride=2 * CH), :] = g[h * qtot : (h + 1) * qtot]
            return carry

        lax.fori_loop(0, hi - lo, one, 0)
        snd[c] = stage[...].astype(jnp.bfloat16).reshape(snd.shape[1:])

    spec_copy.wait()
    leg_copy.wait()
    done = 0
    own = []
    for c in range(chunks):
        upto = rows * (c + 1) // chunks
        basis_rows(done, upto)
        done = upto
        for d in range(1, nl):
            ag(c, d).wait_recv()
        fourier(c)
        for d in range(1, nw):
            aa(c, d).start()
        keep = pltpu.make_async_copy(snd.at[c, wi], rcv.at[c, wi], own_sem.at[c])
        keep.start()
        own.append(keep)

    for c in range(chunks):
        own[c].wait()
        for d in range(1, nw):
            aa(c, d).wait_recv()

    lanes = lax.broadcasted_iota(jnp.int32, (layers, half_width), 1)

    def final(r, carry):
        lat = lat_ref[wi * rows + r]
        half = 10 + 2 * jnp.minimum(lat, NLAT - 1 - lat)
        sums = []
        for par in range(2):
            v = rcv[:, :, r, par].reshape(kdim, 2 * layers)
            vt = v.T
            lhs = jnp.concatenate([vt[:layers], vt[layers:]], axis=1)
            sums.append(jnp.dot(lhs, basis[r, par], preferred_element_type=jnp.float32))
        inside = lanes < half
        first = jnp.where(inside, sums[0] + sums[1], 0.0)
        second = jnp.where(inside, sums[0] - sums[1], 0.0)
        blank = jnp.zeros_like(first)
        moved = pltpu.roll(jnp.concatenate([second, blank], axis=1), half, 1)
        whole = jnp.concatenate([first, blank], axis=1) + moved
        obuf[r] = whole[:, :width].astype(jnp.bfloat16)
        return carry

    lax.fori_loop(0, rows, final, 0)
    out_copy = pltpu.make_async_copy(obuf, out_ref, out_sem)
    out_copy.start()

    for c in range(chunks):
        for d in range(1, nl):
            ag(c, d).wait_send()
        for d in range(1, nw):
            aa(c, d).wait_send()
    out_copy.wait()


def on_device(spectral, legendre, wave_pair, lat_slot):
    slots, fold, items = spectral.shape
    wave_count = fold - 1
    nw = lax.axis_size("wav")
    nl = lax.axis_size("lev")
    rows = lat_slot.shape[0] // nw
    layers = items // 2
    width = 2 * NLAT + 16
    half_width = -(-(width // 2) // LANE) * LANE
    chunks = -(-slots // CH)
    kdim = chunks * nw * CH
    leg_t = jnp.transpose(legendre, (0, 2, 1))
    lrows = leg_t.shape[1]

    pairs = jnp.pad(wave_pair.reshape(nw, slots), ((0, 0), (0, chunks * CH - slots)), constant_values=-1)
    pairs = pairs.reshape(nw, chunks, CH).transpose(1, 0, 2).reshape(kdim)
    m_even = jnp.where(pairs % 2 == 0, pairs, wave_count - 1 - pairs)
    m_even = jnp.where(pairs < 0, -1, m_even).astype(jnp.float32)
    m_even = jnp.broadcast_to(m_even[:, None], (kdim, LANE))
    i = jnp.arange(items)
    perm = (i[:, None] == (2 * (i % layers) + i // layers)[None, :]).astype(jnp.bfloat16)

    vmem = pl.BlockSpec(memory_space=pltpu.VMEM)
    smem = pl.BlockSpec(memory_space=pltpu.SMEM)
    hbm = pl.BlockSpec(memory_space=pl.ANY)
    dma = pltpu.SemaphoreType.DMA
    return pl.pallas_call(
        functools.partial(kernel, nw, nl, slots, wave_count, half_width),
        out_shape=jax.ShapeDtypeStruct((rows, layers, width), jnp.bfloat16),
        in_specs=[smem, smem, vmem, vmem, hbm, hbm],
        out_specs=hbm,
        scratch_shapes=[
            pltpu.VMEM((slots, fold, items), jnp.bfloat16),
            pltpu.VMEM((nl, slots, lrows, fold), jnp.bfloat16),
            pltpu.VMEM((nw * rows * 2 * CH, items), jnp.float32),
            pltpu.VMEM((chunks, nw, rows, 2, CH, items), jnp.bfloat16),
            pltpu.VMEM((chunks, nw, rows, 2, CH, items), jnp.bfloat16),
            pltpu.VMEM((rows, 2, 2 * kdim, half_width), jnp.bfloat16),
            pltpu.VMEM((rows, layers, width), jnp.bfloat16),
            dma((2,)),
            dma((chunks, nl)),
            dma((chunks, nl)),
            dma((chunks, nw)),
            dma((chunks, nw)),
            dma((chunks,)),
            dma,
        ],
        compiler_params=pltpu.CompilerParams(collective_id=0, has_side_effects=True),
    )(wave_pair, lat_slot, m_even, perm, spectral, leg_t)


def solution(mesh):
    return jax.shard_map(
        on_device,
        mesh=mesh,
        in_specs=(P("wav", None, "lev"), P("wav", None, "lev"), P(), P()),
        out_specs=P("wav", "lev", None),
        check_vma=False,
    )
```

time: 259 us -> 68.8 us (0.27)
  the two profiles are of different devices: /device:TPU:1 before, /device:TPU:9 now
where the time goes in v1:
time: 68.8 us; the launch traced here: 68.6 us
  Pallas kernels  63.5 us (92%)
  local copies, waits for them, and re-layouts  4.44 us (6%)
    pallas_call x1, Pallas kernels, on_device(): pl.pallas_call(functools.partial(kernel, nw, nl, slots, wave_count, half_...  63.5 us
    unnamed x1, local copies, waits for them, and re-layouts  2.76 us

profile of v1, /device:TPU:9, one launch (start us, length us, event | category | flops | bytes accessed | tf_op | source)
XLA Modules:
  0.0 68.6 jit_solution(17634877337234461258)
XLA Ops:
  0.0 0.8 %reshape.67 = s32[8,25]{1,0:T(8,128)S(1)} reshape(s32[200]{0:T(256)} %wp_ref.1) | data formatting | bytes 1600 | tf_op jit(solution)/shard_map/reshape | solution.py:212
  0.8 0.1 reshape.68
  0.9 0.1 reshape.69
  1.0 0.6 fusion.perm_ref
  1.6 0.8 %broadcast_in_dim.7.meven_ref = f32[256,128]{1,0:T(8,128)} broadcast(f32[256]{0:T(256)S(1)} %fusion.2), dimensions={0} | broadcast | bytes 132096 | tf_op jit(solution)/shard_map/broadcast_in_dim | solution.py:216
  2.3 63.5 %shard_map.46 = bf16[8,64,1616]{2,1,0:T(8,128)(2,1)} custom-call(s32[200]{0:T(256)} %wp_ref.1, s32[64]{0:T(128)} %lat_ref.1, f32[256,128]{1,0:T(8,128)} %broadcast_in_dim.7.meven_ref, bf16[128,128]{1,0:T(8,128)(2,1)} %fusion.perm_ref, bf16[25,401,128]{2,1,0:T(8,128)(2,1)} %spec_ref.1, bf16[25,16,401]{2,1,0:T(8,128)(2,1)} %bitcast.2), custom_call_target="tpu_custom_call" | custom-call | tf_op jit(solution)/shard_map/pallas_call | solution.py:224
  65.8 2.8 %copy.7 = bf16[8,64,1616]{2,1,0:T(8,128)(2,1)} copy(bf16[8,64,1616]{2,1,0:T(8,128)(2,1)} %shard_map.46) | data formatting | bytes 3309568
  (4 shorter events, 0.0 us)

commit v2 on v1

--- a/solution.py
+++ b/solution.py
@@ -34,8 +34,8 @@
 
 def kernel(
     nw, nl, slots, wave_count, half_width,
-    wp_ref, lat_ref, meven_ref, perm_ref, spec_ref, leg_ref, out_ref,
-    spec, leg, stage, snd, rcv, basis, obuf,
+    wp_ref, lat_ref, spec_ref, leg_ref, out_ref,
+    spec, own, leg, tail, expand, meven, stage, snd, rcv, basis, obuf,
     loc_sem, ag_send, ag_recv, aa_send, aa_recv, own_sem, out_sem,
 ):
     wi = lax.axis_index("wav")
@@ -43,17 +43,25 @@
     chunks = snd.shape[0]
     rows = obuf.shape[0]
     fold = spec.shape[1]
+    main = leg.shape[3]
+    rest = fold - main
+    per_tile = LANE // rest
+    span = (CH // per_tile) * per_tile
     layers = obuf.shape[1]
+    items = 2 * layers
     width = out_ref.shape[2]
     kdim = chunks * nw * CH
     blocks = half_width // LANE
     qtot = nw * rows
     fmt = pl.DeviceIdType.MESH
-
-    spec_copy = pltpu.make_async_copy(spec_ref, spec, loc_sem.at[0])
+    bounds = [(c * span, min(slots, (c + 1) * span)) for c in range(chunks)]
+
+    own_copy = pltpu.make_async_copy(leg_ref, own, loc_sem.at[0])
+    own_copy.start()
+    leg_copy = pltpu.make_async_copy(leg_ref.at[:, :, pl.ds(0, main)], leg.at[li], loc_sem.at[1])
+    leg_copy.start()
+    spec_copy = pltpu.make_async_copy(spec_ref, spec, loc_sem.at[2])
     spec_copy.start()
-    leg_copy = pltpu.make_async_copy(leg_ref, leg.at[li], loc_sem.at[1])
-    leg_copy.start()
 
     barrier = pltpu.get_barrier_semaphore()
     for d in range(1, nl):
@@ -62,16 +70,53 @@
         pl.semaphore_signal(barrier, inc=1, device_id=(lax.rem(wi + d, nw), li), device_id_type=fmt)
     pl.semaphore_wait(barrier, nl - 1 + nw - 1)
 
-    def ag(c, d):
-        lo, hi = c * CH, min(slots, (c + 1) * CH)
+    def hop(way, k, c, part, block):
+        lo, hi = bounds[c]
+        if part == 0:
+            view = leg.at[block, pl.ds(lo, hi - lo)]
+            src = leg_ref.at[pl.ds(lo, hi - lo), :, pl.ds(0, main)] if k == 0 else view
+        else:
+            view = tail.at[block, c]
+            src = view
         return pltpu.make_async_remote_copy(
-            src_ref=leg_ref.at[pl.ds(lo, hi - lo)],
-            dst_ref=leg.at[li, pl.ds(lo, hi - lo)],
-            send_sem=ag_send.at[c, d],
-            recv_sem=ag_recv.at[c, d],
-            device_id=(wi, lax.rem(li + d, nl)),
+            src_ref=src,
+            dst_ref=view,
+            send_sem=ag_send.at[way, k, c, part],
+            recv_sem=ag_recv.at[way, k, c, part],
+            device_id=(wi, li + 1 - 2 * way),
             device_id_type=fmt,
         )
+
+    def sends(way, k):
+        if way == 0:
+            return (li - k >= 0) & (li + 1 < nl), jnp.maximum(li - k, 0)
+        return (li + k < nl) & (li >= 1), jnp.minimum(li + k, nl - 1)
+
+    def receives(way, k):
+        if way == 0:
+            return li - 1 - k >= 0, jnp.maximum(li - 1 - k, 0)
+        return li + 1 + k < nl, jnp.minimum(li + 1 + k, nl - 1)
+
+    def send(k, c, part):
+        for way in range(2):
+            going, block = sends(way, k)
+
+            @pl.when(going)
+            def _():
+                hop(way, k, c, part, block).start()
+
+    def arrive(k, c):
+        for way in range(2):
+            coming, block = receives(way, k)
+
+            @pl.when(coming)
+            def _():
+                hop(way, k, c, 0, block).wait_recv()
+                hop(way, k, c, 1, block).wait_recv()
+
+        if k + 1 < nl - 1:
+            send(k + 1, c, 0)
+            send(k + 1, c, 1)
 
     def aa(c, d):
         dest = lax.rem(wi + d, nw)
@@ -85,8 +130,40 @@
         )
 
     for c in range(chunks):
-        for d in range(1, nl):
-            ag(c, d).start()
+        send(0, c, 0)
+    own_copy.wait()
+    place_t = lax.broadcasted_iota(jnp.int32, (rest, LANE), 0)
+    place_x = lax.broadcasted_iota(jnp.int32, (rest, LANE), 1)
+    for c in range(chunks):
+        lo, hi = bounds[c]
+        for g in range(tail.shape[2]):
+            total = jnp.zeros(tail.shape[3:], jnp.float32)
+            for n in range(per_tile):
+                s = lo + g * per_tile + n
+                if s < hi:
+                    place = jnp.where(place_x == place_t + n * rest, 1.0, 0.0).astype(jnp.bfloat16)
+                    total += jnp.dot(own[s, :, main:], place, preferred_element_type=jnp.float32)
+            tail[li, c, g] = total.astype(jnp.bfloat16)
+        send(0, c, 1)
+
+    meven[...] = jnp.full_like(meven, -1.0)
+
+    def place_pairs(src, carry):
+        for c in range(chunks):
+            lo, hi = bounds[c]
+            for s in range(lo, hi):
+                p = wp_ref[src * slots + s]
+                even = jnp.where(jnp.bitwise_and(p, 1) == 0, p, wave_count - 1 - p)
+                even = jnp.where(p < 0, -1, even).astype(jnp.float32)
+                meven[pl.ds((c * nw + src) * CH + s - lo, 1), :] = jnp.full((1, LANE), even, jnp.float32)
+        return carry
+
+    lax.fori_loop(0, nw, place_pairs, 0)
+    out_i = lax.broadcasted_iota(jnp.int32, (items, items), 1)
+    in_i = lax.broadcasted_iota(jnp.int32, (items, items), 0)
+    perm = jnp.where(
+        in_i == jnp.where(out_i < layers, 2 * out_i, 2 * (out_i - layers) + 1), 1.0, 0.0
+    ).astype(jnp.bfloat16)
 
     fine = lax.broadcasted_iota(jnp.int32, (KB, LANE), 1).astype(jnp.float32)
 
@@ -98,7 +175,7 @@
         highest = jnp.minimum(wave_count - 1, lax.shift_right_logical(count_i - 1, 1)).astype(jnp.float32)
         count = jnp.full((KB, LANE), count_i.astype(jnp.float32), jnp.float32)
         inv = 1.0 / count
-        m_even = meven_ref[pl.ds(k0, KB), :]
+        m_even = meven[pl.ds(k0, KB), :]
         for par in range(2):
             m = m_even if par == 0 else (wave_count - 1.0) - m_even
             amp = jnp.where((m >= 0.0) & (m <= highest), jnp.where(m == 0.0, 1.0, 2.0), 0.0)
@@ -118,22 +195,46 @@
         lax.fori_loop(lo * (kdim // KB), hi * (kdim // KB), make_basis, 0)
 
     stage[...] = jnp.zeros_like(stage)
-    cols = lax.broadcasted_iota(jnp.int32, (1, fold), 1)
+    cols = lax.broadcasted_iota(jnp.int32, (1, main), 1)
+    tcols = lax.broadcasted_iota(jnp.int32, (1, LANE), 1)
+    back_x = lax.broadcasted_iota(jnp.int32, (LANE, rest), 0)
+    back_t = lax.broadcasted_iota(jnp.int32, (LANE, rest), 1)
+
+    spec_copy.wait()
+    for c in range(chunks):
+        lo, hi = bounds[c]
+
+        def widen(i, carry):
+            n = lax.rem(i, per_tile)
+            back = jnp.where(back_x == back_t + n * rest, 1.0, 0.0).astype(jnp.bfloat16)
+            expand[lo + i] = jnp.dot(
+                back, spec[lo + i, main:, :], preferred_element_type=jnp.float32
+            ).astype(jnp.bfloat16)
+            return carry
+
+        lax.fori_loop(0, hi - lo, widen, 0)
 
     def fourier(c):
-        lo, hi = c * CH, min(slots, (c + 1) * CH)
+        lo, hi = bounds[c]
 
         def one(i, carry):
             s = lo + i
             p = wp_ref[wi * slots + s]
-            low = jnp.where(cols < wave_count - p, 1, 0)
             par = jnp.bitwise_and(p, 1)
-            even = jnp.where(low != par, 1.0, 0.0).astype(jnp.bfloat16)
-            lg = leg[:, pl.ds(s, 1)].reshape(qtot, fold)
-            lg_even = lg * even
-            both = jnp.concatenate([lg_even, lg - lg_even], axis=0)
-            f = jnp.dot(both, spec[s], preferred_element_type=jnp.float32).astype(jnp.bfloat16)
-            g = jnp.dot(f, perm_ref[...], preferred_element_type=jnp.float32)
+            border = wave_count - p
+
+            def split(values, fold_rows):
+                low = jnp.where(fold_rows < border, 1, 0)
+                even = jnp.where(low != par, 1.0, 0.0).astype(jnp.bfloat16)
+                picked = values * even
+                return jnp.concatenate([picked, values - picked], axis=0)
+
+            lg = split(leg[:, pl.ds(s, 1)].reshape(qtot, main), cols)
+            tile = tail[:, c, pl.ds(lax.div(i, per_tile), 1)].reshape(qtot, LANE)
+            lt = split(tile, main + tcols - lax.rem(i, per_tile) * rest)
+            f = jnp.dot(lg, spec[s, :main, :], preferred_element_type=jnp.float32)
+            f = f + jnp.dot(lt, expand[s], preferred_element_type=jnp.float32)
+            g = jnp.dot(f.astype(jnp.bfloat16), perm, preferred_element_type=jnp.float32)
             for h in range(2):
                 stage[pl.ds(h * CH + i, qtot, stride=2 * CH), :] = g[h * qtot : (h + 1) * qtot]
             return carry
@@ -141,25 +242,28 @@
         lax.fori_loop(0, hi - lo, one, 0)
         snd[c] = stage[...].astype(jnp.bfloat16).reshape(snd.shape[1:])
 
-    spec_copy.wait()
     leg_copy.wait()
+    polls = [(k, c) for k in range(nl - 1) for c in range(chunks)]
+    early = len(polls) - chunks
     done = 0
-    own = []
-    for c in range(chunks):
-        upto = rows * (c + 1) // chunks
+    for n, (k, c) in enumerate(polls[:early]):
+        upto = rows * (n + 1) // (early + 1)
         basis_rows(done, upto)
         done = upto
-        for d in range(1, nl):
-            ag(c, d).wait_recv()
+        arrive(k, c)
+    basis_rows(done, rows)
+    keeps = []
+    for c in range(chunks):
+        arrive(nl - 2, c)
         fourier(c)
         for d in range(1, nw):
             aa(c, d).start()
         keep = pltpu.make_async_copy(snd.at[c, wi], rcv.at[c, wi], own_sem.at[c])
         keep.start()
-        own.append(keep)
-
-    for c in range(chunks):
-        own[c].wait()
+        keeps.append(keep)
+
+    for c in range(chunks):
+        keeps[c].wait()
         for d in range(1, nw):
             aa(c, d).wait_recv()
 
@@ -188,8 +292,15 @@
     out_copy.start()
 
     for c in range(chunks):
-        for d in range(1, nl):
-            ag(c, d).wait_send()
+        for k in range(nl - 1):
+            for way in range(2):
+                going, block = sends(way, k)
+
+                @pl.when(going)
+                def _():
+                    for part in range(2):
+                        hop(way, k, c, part, block).wait_send()
+
         for d in range(1, nw):
             aa(c, d).wait_send()
     out_copy.wait()
@@ -204,46 +315,46 @@
     layers = items // 2
     width = 2 * NLAT + 16
     half_width = -(-(width // 2) // LANE) * LANE
-    chunks = -(-slots // CH)
+    main = fold // LANE * LANE
+    per_tile = LANE // (fold - main)
+    span = (CH // per_tile) * per_tile
+    chunks = -(-slots // span)
     kdim = chunks * nw * CH
     leg_t = jnp.transpose(legendre, (0, 2, 1))
     lrows = leg_t.shape[1]
 
-    pairs = jnp.pad(wave_pair.reshape(nw, slots), ((0, 0), (0, chunks * CH - slots)), constant_values=-1)
-    pairs = pairs.reshape(nw, chunks, CH).transpose(1, 0, 2).reshape(kdim)
-    m_even = jnp.where(pairs % 2 == 0, pairs, wave_count - 1 - pairs)
-    m_even = jnp.where(pairs < 0, -1, m_even).astype(jnp.float32)
-    m_even = jnp.broadcast_to(m_even[:, None], (kdim, LANE))
-    i = jnp.arange(items)
-    perm = (i[:, None] == (2 * (i % layers) + i // layers)[None, :]).astype(jnp.bfloat16)
-
-    vmem = pl.BlockSpec(memory_space=pltpu.VMEM)
     smem = pl.BlockSpec(memory_space=pltpu.SMEM)
     hbm = pl.BlockSpec(memory_space=pl.ANY)
     dma = pltpu.SemaphoreType.DMA
+    vmem = pltpu.VMEM
+    half = jnp.bfloat16
     return pl.pallas_call(
         functools.partial(kernel, nw, nl, slots, wave_count, half_width),
-        out_shape=jax.ShapeDtypeStruct((rows, layers, width), jnp.bfloat16),
-        in_specs=[smem, smem, vmem, vmem, hbm, hbm],
+        out_shape=jax.ShapeDtypeStruct((rows, layers, width), half),
+        in_specs=[smem, smem, hbm, hbm],
         out_specs=hbm,
         scratch_shapes=[
-            pltpu.VMEM((slots, fold, items), jnp.bfloat16),
-            pltpu.VMEM((nl, slots, lrows, fold), jnp.bfloat16),
-            pltpu.VMEM((nw * rows * 2 * CH, items), jnp.float32),
-            pltpu.VMEM((chunks, nw, rows, 2, CH, items), jnp.bfloat16),
-            pltpu.VMEM((chunks, nw, rows, 2, CH, items), jnp.bfloat16),
-            pltpu.VMEM((rows, 2, 2 * kdim, half_width), jnp.bfloat16),
-            pltpu.VMEM((rows, layers, width), jnp.bfloat16),
-            dma((2,)),
-            dma((chunks, nl)),
-            dma((chunks, nl)),
+            vmem((slots, fold, items), half),
+            vmem((slots, lrows, fold), half),
+            vmem((nl, slots, lrows, main), half),
+            vmem((nl, chunks, CH // per_tile, lrows, LANE), half),
+            vmem((slots, LANE, items), half),
+            vmem((kdim, LANE), jnp.float32),
+            vmem((nw * rows * 2 * CH, items), jnp.float32),
+            vmem((chunks, nw, rows, 2, CH, items), half),
+            vmem((chunks, nw, rows, 2, CH, items), half),
+            vmem((rows, 2, 2 * kdim, half_width), half),
+            vmem((rows, layers, width), half),
+            dma((3,)),
+            dma((2, nl - 1, chunks, 2)),
+            dma((2, nl - 1, chunks, 2)),
             dma((chunks, nw)),
             dma((chunks, nw)),
             dma((chunks,)),
             dma,
         ],
         compiler_params=pltpu.CompilerParams(collective_id=0, has_side_effects=True),
-    )(wave_pair, lat_slot, m_even, perm, spectral, leg_t)
+    )(wave_pair, lat_slot, spectral, leg_t)
 
 
 def solution(mesh):

time: 68.8 us -> 52.8 us (0.77)
  the two profiles are of different devices: /device:TPU:9 before, /device:TPU:1 now
where the time goes in v2:
time: 52.8 us; the launch traced here: 52.6 us
  Pallas kernels  49.9 us (95%)
  local copies, waits for them, and re-layouts  2.76 us (5%)
    pallas_call x1, Pallas kernels, on_device(): pl.pallas_call(functools.partial(kernel, nw, nl, slots, wave_count, half_...  49.9 us
    unnamed x1, local copies, waits for them, and re-layouts  2.76 us

profile of v2, /device:TPU:1, one launch (start us, length us, event | category | flops | bytes accessed | tf_op | source)
XLA Modules:
  0.0 52.6 jit_solution(6693307346399038672)
XLA Ops:
  0.0 49.9 %shard_map.46 = bf16[8,64,1616]{2,1,0:T(8,128)(2,1)} custom-call(s32[200]{0:T(256)} %wp_ref.1, s32[64]{0:T(128)} %lat_ref.1, bf16[25,401,128]{2,1,0:T(8,128)(2,1)} %spec_ref.1, bf16[25,16,401]{2,1,0:T(8,128)(2,1)} %bitcast.1), custom_call_target="tpu_custom_call" | custom-call | tf_op jit(solution)/shard_map/pallas_call | solution.py:331
  49.9 2.8 %copy.6 = bf16[8,64,1616]{2,1,0:T(8,128)(2,1)} copy(bf16[8,64,1616]{2,1,0:T(8,128)(2,1)} %shard_map.46) | data formatting | bytes 3309568

commit v3 on v2

--- a/solution.py
+++ b/solution.py
@@ -35,7 +35,7 @@
 def kernel(
     nw, nl, slots, wave_count, half_width,
     wp_ref, lat_ref, spec_ref, leg_ref, out_ref,
-    spec, own, leg, tail, expand, meven, stage, snd, rcv, basis, obuf,
+    spec, own, leg, tail, expand, meven, amp, full, part, stage, snd, rcv, basis, obuf,
     loc_sem, ag_send, ag_recv, aa_send, aa_recv, own_sem, out_sem,
 ):
     wi = lax.axis_index("wav")
@@ -70,9 +70,9 @@
         pl.semaphore_signal(barrier, inc=1, device_id=(lax.rem(wi + d, nw), li), device_id_type=fmt)
     pl.semaphore_wait(barrier, nl - 1 + nw - 1)
 
-    def hop(way, k, c, part, block):
+    def hop(way, k, c, piece, block):
         lo, hi = bounds[c]
-        if part == 0:
+        if piece == 0:
             view = leg.at[block, pl.ds(lo, hi - lo)]
             src = leg_ref.at[pl.ds(lo, hi - lo), :, pl.ds(0, main)] if k == 0 else view
         else:
@@ -81,8 +81,8 @@
         return pltpu.make_async_remote_copy(
             src_ref=src,
             dst_ref=view,
-            send_sem=ag_send.at[way, k, c, part],
-            recv_sem=ag_recv.at[way, k, c, part],
+            send_sem=ag_send.at[way, k, c, piece],
+            recv_sem=ag_recv.at[way, k, c, piece],
             device_id=(wi, li + 1 - 2 * way),
             device_id_type=fmt,
         )
@@ -97,13 +97,13 @@
             return li - 1 - k >= 0, jnp.maximum(li - 1 - k, 0)
         return li + 1 + k < nl, jnp.minimum(li + 1 + k, nl - 1)
 
-    def send(k, c, part):
+    def send(k, c, piece):
         for way in range(2):
             going, block = sends(way, k)
 
             @pl.when(going)
             def _():
-                hop(way, k, c, part, block).start()
+                hop(way, k, c, piece, block).start()
 
     def arrive(k, c):
         for way in range(2):
@@ -166,33 +166,61 @@
     ).astype(jnp.bfloat16)
 
     fine = lax.broadcasted_iota(jnp.int32, (KB, LANE), 1).astype(jnp.float32)
+    ahead = lax.broadcasted_iota(jnp.int32, (8, half_width), 1).astype(jnp.float32)
+    kchunk = nw * CH
+    pieces = kdim // KB
+
+    def turn(x, y):
+        return x[0] * y[0] - x[1] * y[1], x[0] * y[1] + x[1] * y[0]
+
+    def minus(pair):
+        return pair[0], -pair[1]
+
+    def row_count(r):
+        lat = lat_ref[wi * rows + r]
+        return 20 + 4 * jnp.minimum(lat, NLAT - 1 - lat)
 
     def make_basis(step, carry):
-        r = lax.div(step, kdim // KB)
-        k0 = pl.multiple_of(lax.rem(step, kdim // KB) * KB, KB)
-        lat = lat_ref[wi * rows + r]
-        count_i = 20 + 4 * jnp.minimum(lat, NLAT - 1 - lat)
+        r = lax.div(step, pieces)
+        k0 = pl.multiple_of(lax.rem(step, pieces) * KB, KB)
+        slab = lax.div(k0, kchunk)
+        real = pl.multiple_of(k0 + slab * kchunk, KB)
+        imag = pl.multiple_of(real + kchunk, KB)
+        count_i = row_count(r)
         highest = jnp.minimum(wave_count - 1, lax.shift_right_logical(count_i - 1, 1)).astype(jnp.float32)
         count = jnp.full((KB, LANE), count_i.astype(jnp.float32), jnp.float32)
         inv = 1.0 / count
         m_even = meven[pl.ds(k0, KB), :]
         for par in range(2):
             m = m_even if par == 0 else (wave_count - 1.0) - m_even
-            amp = jnp.where((m >= 0.0) & (m <= highest), jnp.where(m == 0.0, 1.0, 2.0), 0.0)
-            cf, sf = trig(m * fine, count, inv)
-            cc, sc = trig(m * (fine * LANE), count, inv)
-            cc = cc * amp
-            sc = sc * amp
-            for b in range(blocks):
-                cb = cc[:, b : b + 1]
-                sb = sc[:, b : b + 1]
-                cols = slice(b * LANE, (b + 1) * LANE)
-                basis[r, par, pl.ds(k0, KB), cols] = (cb * cf - sb * sf).astype(jnp.bfloat16)
-                basis[r, par, pl.ds(kdim + k0, KB), cols] = (-(sb * cf + cb * sf)).astype(jnp.bfloat16)
+            factor = jnp.where((m >= 0.0) & (m <= highest), jnp.where(m == 0.0, 1.0, 2.0), 0.0)
+            amp[r, par, pl.ds(k0, KB), :] = factor.astype(jnp.bfloat16)
+        now = minus(trig(m_even * fine, count, inv))
+        stride = minus(trig(m_even * LANE, count, inv))
+        for b in range(blocks):
+            cols = slice(b * LANE, (b + 1) * LANE)
+            if b:
+                now = turn(now, stride)
+            c4 = jnp.broadcast_to(full[r, 0, 0:1, cols], (KB, LANE))
+            s4 = jnp.broadcast_to(full[r, 1, 0:1, cols], (KB, LANE))
+            basis[r, 0, pl.ds(real, KB), cols] = now[0].astype(jnp.bfloat16)
+            basis[r, 0, pl.ds(imag, KB), cols] = now[1].astype(jnp.bfloat16)
+            other = (c4 * now[0] + s4 * now[1], s4 * now[0] - c4 * now[1])
+            basis[r, 1, pl.ds(real, KB), cols] = other[0].astype(jnp.bfloat16)
+            basis[r, 1, pl.ds(imag, KB), cols] = other[1].astype(jnp.bfloat16)
         return carry
 
+    def make_full(r, carry):
+        count = jnp.full((8, half_width), row_count(r).astype(jnp.float32), jnp.float32)
+        cos_full, neg_sin_full = minus(trig((wave_count - 1.0) * ahead, count, 1.0 / count))
+        full[r, 0] = cos_full
+        full[r, 1] = neg_sin_full
+        return carry
+
+    lax.fori_loop(0, rows, make_full, 0)
+
     def basis_rows(lo, hi):
-        lax.fori_loop(lo * (kdim // KB), hi * (kdim // KB), make_basis, 0)
+        lax.fori_loop(lo * pieces, hi * pieces, make_basis, 0)
 
     stage[...] = jnp.zeros_like(stage)
     cols = lax.broadcasted_iota(jnp.int32, (1, main), 1)
@@ -217,7 +245,7 @@
     def fourier(c):
         lo, hi = bounds[c]
 
-        def one(i, carry):
+        for i in range(hi - lo):
             s = lo + i
             p = wp_ref[wi * slots + s]
             par = jnp.bitwise_and(p, 1)
@@ -229,17 +257,15 @@
                 picked = values * even
                 return jnp.concatenate([picked, values - picked], axis=0)
 
-            lg = split(leg[:, pl.ds(s, 1)].reshape(qtot, main), cols)
-            tile = tail[:, c, pl.ds(lax.div(i, per_tile), 1)].reshape(qtot, LANE)
-            lt = split(tile, main + tcols - lax.rem(i, per_tile) * rest)
+            lg = split(leg[:, s].reshape(qtot, main), cols)
+            tile = tail[:, c, i // per_tile].reshape(qtot, LANE)
+            lt = split(tile, main + tcols - i % per_tile * rest)
             f = jnp.dot(lg, spec[s, :main, :], preferred_element_type=jnp.float32)
             f = f + jnp.dot(lt, expand[s], preferred_element_type=jnp.float32)
             g = jnp.dot(f.astype(jnp.bfloat16), perm, preferred_element_type=jnp.float32)
             for h in range(2):
                 stage[pl.ds(h * CH + i, qtot, stride=2 * CH), :] = g[h * qtot : (h + 1) * qtot]
-            return carry
-
-        lax.fori_loop(0, hi - lo, one, 0)
+
         snd[c] = stage[...].astype(jnp.bfloat16).reshape(snd.shape[1:])
 
     leg_copy.wait()
@@ -262,22 +288,39 @@
         keep.start()
         keeps.append(keep)
 
-    for c in range(chunks):
+    def landed(c):
         keeps[c].wait()
         for d in range(1, nw):
             aa(c, d).wait_recv()
 
+    def product(c, r, par):
+        weight = amp[r, par, c * kchunk : (c + 1) * kchunk, :]
+        v = rcv[c, :, r, par].reshape(kchunk, items) * weight
+        vt = v.T
+        lhs = jnp.concatenate([vt[:layers], vt[layers:]], axis=1)
+        rhs = basis[r, par, 2 * c * kchunk : 2 * (c + 1) * kchunk, :]
+        return jnp.dot(lhs, rhs, preferred_element_type=jnp.float32)
+
+    for c in range(chunks - 1):
+        landed(c)
+
+        def partial(r, carry):
+            for par in range(2):
+                value = product(c, r, par)
+                part[r, par] = value if c == 0 else part[r, par] + value
+            return carry
+
+        lax.fori_loop(0, rows, partial, 0)
+
     lanes = lax.broadcasted_iota(jnp.int32, (layers, half_width), 1)
+    landed(chunks - 1)
 
     def final(r, carry):
-        lat = lat_ref[wi * rows + r]
-        half = 10 + 2 * jnp.minimum(lat, NLAT - 1 - lat)
+        half = lax.shift_right_logical(row_count(r), 1)
         sums = []
         for par in range(2):
-            v = rcv[:, :, r, par].reshape(kdim, 2 * layers)
-            vt = v.T
-            lhs = jnp.concatenate([vt[:layers], vt[layers:]], axis=1)
-            sums.append(jnp.dot(lhs, basis[r, par], preferred_element_type=jnp.float32))
+            value = product(chunks - 1, r, par)
+            sums.append(value if chunks == 1 else part[r, par] + value)
         inside = lanes < half
         first = jnp.where(inside, sums[0] + sums[1], 0.0)
         second = jnp.where(inside, sums[0] - sums[1], 0.0)
@@ -298,8 +341,8 @@
 
                 @pl.when(going)
                 def _():
-                    for part in range(2):
-                        hop(way, k, c, part, block).wait_send()
+                    for piece in range(2):
+                        hop(way, k, c, piece, block).wait_send()
 
         for d in range(1, nw):
             aa(c, d).wait_send()
@@ -340,6 +383,9 @@
             vmem((nl, chunks, CH // per_tile, lrows, LANE), half),
             vmem((slots, LANE, items), half),
             vmem((kdim, LANE), jnp.float32),
+            vmem((rows, 2, kdim, LANE), half),
+            vmem((rows, 2, 8, half_width), jnp.float32),
+            vmem((rows, 2, layers, half_width), jnp.float32),
             vmem((nw * rows * 2 * CH, items), jnp.float32),
             vmem((chunks, nw, rows, 2, CH, items), half),
             vmem((chunks, nw, rows, 2, CH, items), half),

time: 52.8 us -> 49 us (0.928)
  Pallas kernels: 49.9 us -> 46.1 us
    pallas_call x1, Pallas kernels: 49.9 us -> 46.1 us  [on_device(): pl.pallas_call(functools.partial(kernel, nw, nl, slots, wave_count, half_...]
where the time goes in v3:
time: 49 us; the launch traced here: 48.8 us
  Pallas kernels  46.1 us (94%)
  local copies, waits for them, and re-layouts  2.76 us (6%)
    pallas_call x1, Pallas kernels, on_device(): pl.pallas_call(functools.partial(kernel, nw, nl, slots, wave_count, half_...  46.1 us
    unnamed x1, local copies, waits for them, and re-layouts  2.76 us

profile of v3, /device:TPU:1, one launch (start us, length us, event | category | flops | bytes accessed | tf_op | source)
XLA Modules:
  0.0 48.8 jit_solution(1522877790267202408)
XLA Ops:
  0.0 46.1 %shard_map.46 = bf16[8,64,1616]{2,1,0:T(8,128)(2,1)} custom-call(s32[200]{0:T(256)} %wp_ref.1, s32[64]{0:T(128)} %lat_ref.1, bf16[25,401,128]{2,1,0:T(8,128)(2,1)} %spec_ref.1, bf16[25,16,401]{2,1,0:T(8,128)(2,1)} %bitcast.1), custom_call_target="tpu_custom_call" | custom-call | tf_op jit(solution)/shard_map/pallas_call | solution.py:374
  46.1 2.8 %copy.6 = bf16[8,64,1616]{2,1,0:T(8,128)(2,1)} copy(bf16[8,64,1616]{2,1,0:T(8,128)(2,1)} %shard_map.46) | data formatting | bytes 3309568
